TPU v7x, 32 devices: a whole 2x2x4 slice. The times are simulated.
32 devices in a mesh: dp: 2 (over y), seq: 16 (over z, x, core).
Axes of the slice: x: 2, y: 2, z: 4, core: 2. Of those that a mesh axis runs over, the one named last changes fastest.
Arguments:
- features: bfloat16 [4096, 320], P(('dp', 'seq')), parts along dimension 0, may hold values from -40 to 40
- hint: bfloat16 [4096, 320], P(('dp', 'seq')), parts along dimension 0, may hold values from -6 to 6
- conv_weight: bfloat16 [3, 3, 320, 320], replicated, may hold values from -0.109375 to 0.109375
- conv_bias: float32 [320], replicated, may hold values from -3 to 3
- zero_weight: bfloat16 [320, 320], replicated, may hold values from -0.3125 to 0.3125
- zero_bias: float32 [320], replicated, may hold values from -2 to 2
- group_gain: float32 [320], replicated, may hold values from 0.5 to 1.5
- proj_in: bfloat16 [320, 320], replicated, may hold values from -0.3125 to 0.3125
- norm_gain: float32 [320], replicated, may hold values from 0.5 to 1.5
- query_weight: bfloat16 [320, 320], replicated, may hold values from -2 to 2
- key_weight: bfloat16 [320, 320], replicated, may hold values from -2 to 2
- value_weight: bfloat16 [320, 320], replicated, may hold values from -0.3125 to 0.3125
- attn_out: bfloat16 [320, 320], replicated, may hold values from -0.3125 to 0.3125
- proj_out: bfloat16 [320, 320], replicated, may hold values from -0.3125 to 0.3125
Outputs:
- block_out: bfloat16 [4096, 320], P(('dp', 'seq')), parts along dimension 0
There are 2 independent parts, one for each index of `dp`. A program takes and returns all parts, laid end to end along the dimension named above; an argument that names none is the same for every part. Nothing has to cross between parts.
All inputs are finite; a program needn't handle non-finite values.
Results may differ from a plain program's by a relative error of at most 0.023.
Values may be sent and summed in bfloat16 or wider, within the bound.
A program may use at most 64 MiB of HBM per device.

v0:
```python
import math
import jax
import jax.numpy as jnp
from jax import lax
from jax.sharding import PartitionSpec as P

HEADS = 8
GROUPS = 32
WIDTH = 128
norm_eps = 1e-06
layer_eps = 1e-05


def with_halo(block, sides, width):
    for axis, dim in sides:
        count = lax.axis_size(axis)
        forward = [(i, i + 1) for i in range(count - 1)]
        backward = [(target, source) for source, target in forward]
        low = lax.ppermute(
            lax.slice_in_dim(block, block.shape[dim] - width, None, axis=dim), axis, forward
        )
        high = lax.ppermute(lax.slice_in_dim(block, 0, width, axis=dim), axis, backward)
        block = jnp.concatenate([low, block, high], axis=dim)
    return block


def conv_extended(extended, conv_weight, conv_bias, width):
    line_count = extended.shape[0] // width - 2
    channels = extended.shape[1]
    lattice = extended.reshape(line_count + 2, width, channels)
    padded = jnp.pad(lattice, ((0, 0), (1, 1), (0, 0)))
    summed = jnp.zeros((line_count * width, conv_weight.shape[3]), jnp.float32)
    for row_shift in range(3):
        for col_shift in range(3):
            window = padded[row_shift : row_shift + line_count, col_shift : col_shift + width]
            window = window.reshape(line_count * width, channels)
            summed = summed + jnp.dot(
                window, conv_weight[row_shift, col_shift], preferred_element_type=jnp.float32
            )
    return summed + conv_bias


def fold_blocks(carry_in, queries, pieces, make_pairs):
    row_total = pieces[0].shape[0]
    block_len = math.gcd(row_total, 1024)
    stacked = tuple(
        (member.reshape(row_total // block_len, block_len, member.shape[1]) for member in pieces)
    )
    score_scale = 1.0 / math.sqrt(queries.shape[2])

    def advance(carry_now, slab_rows):
        running_max, running_sum, weighted = carry_now
        keys_block, values_block = make_pairs(slab_rows)
        scores = (
            jnp.einsum("qhd,khd->hqk", queries, keys_block, preferred_element_type=jnp.float32)
            * score_scale
        )
        new_max = jnp.maximum(running_max, jnp.max(scores, axis=2))
        decay_by = jnp.exp(running_max - new_max)
        weights = jnp.exp(scores - new_max[:, :, None])
        running_sum = running_sum * decay_by + jnp.sum(weights, axis=2)
        weighted = weighted * jnp.transpose(decay_by)[:, :, None] + jnp.einsum(
            "hqk,khd->qhd",
            weights.astype(jnp.bfloat16),
            values_block,
            preferred_element_type=jnp.float32,
        )
        return ((new_max, running_sum, weighted), None)

    carry_out, unused = lax.scan(advance, carry_in, stacked)
    return carry_out


def local(
    features,
    hint,
    conv_weight,
    conv_bias,
    zero_weight,
    zero_bias,
    group_gain,
    proj_in,
    norm_gain,
    query_weight,
    key_weight,
    value_weight,
    attn_out,
    proj_out,
):
    tok_count, channels = features.shape
    head_dim = channels // HEADS
    extended = with_halo(hint, (("seq", 0),), WIDTH)
    control = jax.nn.silu(conv_extended(extended, conv_weight, conv_bias, WIDTH)).astype(
        jnp.bfloat16
    )
    branch = jnp.dot(control, zero_weight, preferred_element_type=jnp.float32) + zero_bias
    merged = (features.astype(jnp.float32) + branch).astype(jnp.bfloat16)
    widened = merged.astype(jnp.float32)
    per_group = channels // GROUPS
    entry_count = tok_count * lax.axis_size("seq") * per_group
    local_sum = jnp.sum(widened.reshape(tok_count, GROUPS, per_group), axis=(0, 2))
    mean_group = lax.psum(local_sum, "seq") / entry_count
    centred = widened - jnp.repeat(mean_group, per_group)
    local_spread = jnp.sum(jnp.square(centred).reshape(tok_count, GROUPS, per_group), axis=(0, 2))
    var_group = lax.psum(local_spread, "seq") / entry_count
    mean_chan = jnp.repeat(mean_group, per_group)
    inv_chan = jnp.repeat(lax.rsqrt(var_group + norm_eps), per_group)
    grouped = ((widened - mean_chan) * inv_chan * group_gain).astype(jnp.bfloat16)
    inner_rows = jnp.dot(grouped, proj_in, preferred_element_type=jnp.float32).astype(jnp.bfloat16)
    inner_wide = inner_rows.astype(jnp.float32)
    centre = jnp.mean(inner_wide, axis=1, keepdims=True)
    spread = jnp.mean(jnp.square(inner_wide - centre), axis=1, keepdims=True)
    normed = ((inner_wide - centre) * lax.rsqrt(spread + layer_eps) * norm_gain).astype(
        jnp.bfloat16
    )
    queries = jnp.dot(normed, query_weight, preferred_element_type=jnp.float32).astype(jnp.bfloat16)
    queries = queries.reshape(tok_count, HEADS, head_dim)
    group_span = lax.axis_size("seq") // HEADS
    sub_rows = tok_count // group_span
    local_keys = jnp.dot(normed, key_weight, preferred_element_type=jnp.float32).astype(
        jnp.bfloat16
    )
    local_values = jnp.dot(normed, value_weight, preferred_element_type=jnp.float32).astype(
        jnp.bfloat16
    )
    query_send = (
        queries.reshape(group_span, sub_rows, HEADS, head_dim)
        .transpose(2, 0, 1, 3)
        .reshape(HEADS * group_span, sub_rows, head_dim)
    )

    def copies_for(matrix):
        by_head = matrix.reshape(tok_count, HEADS, head_dim).transpose(1, 0, 2)
        return jnp.broadcast_to(by_head[:, None], (HEADS, group_span, tok_count, head_dim)).reshape(
            HEADS * group_span, tok_count, head_dim
        )

    own_queries = lax.all_to_all(query_send, "seq", split_axis=0, concat_axis=0, tiled=True)
    head_keys, head_values = (
        lax.all_to_all(copies_for(local_keys), "seq", split_axis=0, concat_axis=0, tiled=True),
        lax.all_to_all(copies_for(local_values), "seq", split_axis=0, concat_axis=0, tiled=True),
    )
    query_rows = own_queries.shape[0] * sub_rows
    own_queries = own_queries.reshape(query_rows, 1, head_dim)
    key_rows = head_keys.reshape(-1, head_dim)
    value_rows = head_values.reshape(-1, head_dim)

    def single_pairs(slab_rows):
        return (slab_rows[0].reshape(-1, 1, head_dim), slab_rows[1].reshape(-1, 1, head_dim))

    head_carry = (
        jnp.full((1, query_rows), -1e30, jnp.float32),
        jnp.zeros((1, query_rows), jnp.float32),
        jnp.zeros((query_rows, 1, head_dim), jnp.float32),
    )
    running_max, running_sum, weighted = fold_blocks(
        head_carry, own_queries, (key_rows, value_rows), single_pairs
    )
    head_result = (weighted / jnp.transpose(running_sum)[:, :, None]).astype(jnp.bfloat16)
    head_result = head_result.reshape(lax.axis_size("seq"), sub_rows, head_dim)
    returned = lax.all_to_all(head_result, "seq", split_axis=0, concat_axis=0, tiled=True)
    attended = (
        returned.reshape(HEADS, group_span, sub_rows, head_dim)
        .transpose(1, 2, 0, 3)
        .reshape(tok_count, channels)
    )
    after_attn = (
        inner_wide + jnp.dot(attended, attn_out, preferred_element_type=jnp.float32)
    ).astype(jnp.bfloat16)
    return (widened + jnp.dot(after_attn, proj_out, preferred_element_type=jnp.float32)).astype(
        jnp.bfloat16
    )


def solution(mesh):
    placed = (
        P(("dp", "seq"), None),
        P(("dp", "seq"), None),
        P(),
        P(),
        P(),
        P(),
        P(),
        P(),
        P(),
        P(),
        P(),
        P(),
        P(),
        P(),
    )
    return jax.shard_map(
        local, mesh=mesh, in_specs=placed, out_specs=P(("dp", "seq"), None), check_vma=False
    )
```

profile of v0, /device:TPU:0, one launch (start us, length us, event | category | flops | bytes accessed | tf_op | source)
XLA Modules:
  0.0 143.6 jit_solution(5059006337217862261)
XLA Ops:
  0.0 2.7 %collective-permute-start = (bf16[128,320]{0,1:T(8,128)(2,1)}, bf16[128,320]{0,1:T(8,128)(2,1)S(1)}, u32[]{:S(2)}, u32[]{:S(2)}) collective-permute-start(bf16[128,320]{0,1:T(8,128)(2,1)} %param.17), channel_id=1, source_target_pairs={{0,1},{1,2},{2,3},{3,4},{4,5},{5,6},{6,7},{7,8},{8,9},{9,10},{10,1... | collective-permute-start | bytes 245768 | tf_op jit(solution)/shard_map/ppermute | solution.py:19
  2.7 1.3 collective-permute-start.1
  4.0 4.2 %collective-permute-done.1 = bf16[128,320]{0,1:T(8,128)(2,1)S(1)} collective-permute-done((bf16[128,320]{0,1:T(8,128)(2,1)}, bf16[128,320]{0,1:T(8,128)(2,1)S(1)}, u32[]{:S(2)}, u32[]{:S(2)}) %collective-permute-start.1) | collective-permute-done | bytes 81952 | tf_op jit(solution)/shard_map/ppermute | solution.py:22
  8.1 1.0 pad_maximum_fusion
  9.1 0.0 copy-start.3
  9.1 0.2 copy.64
  9.3 1.2 fusion.39
  10.6 1.9 %fusion.30 = f32[128,320]{0,1:T(8,128)} fusion(bf16[3,3,320,320]{3,2,1,0:T(8,128)(2,1)} %param.18, bf16[3,128,320]{2,1,0:T(8,128)(2,1)S(1)} %bitcast.143), kind=kOutput, calls=%fused_computation.46 | convolution fusion | flops 26214400 | bytes 655360 | tf_op jit(solution)/shard_map/dot_general | solution.py:37
  12.5 0.3 convolution_add_fusion.9
  12.8 0.0 copy-start.13
  12.8 0.3 convolution_add_fusion.8
  13.1 0.3 convolution_add_fusion.7
  13.4 0.0 copy-start.4
  13.4 0.3 convolution_add_fusion.6
  13.7 0.3 convolution_add_fusion.5
  14.0 0.9 convolution_add_fusion.4
  15.0 1.7 %fusion.78 = (f32[320]{0:T(512)S(1)}, f32[128,320]{0,1:T(8,128)S(1)}) fusion(f32[320]{0:T(512)S(1)} %copy-done.13, bf16[320,320]{1,0:T(8,128)(2,1)S(1)} %copy-done, f32[128,320]{0,1:T(8,128)} %fusion.30, f32[128,320]{0,1:T(8,128)} %convolution_add_fusion.4, bf16[128,320]{0,1:T(8,128)(2,1)} %copy-done.10, bf16[3,3,320,320]{3,2,1,0:T(8,128)(2,1)S(1)} %copy-done.2, ...), kind=kOutput, calls=%fused_computation.100 | convolution fusion | flops 53001920 | bytes 1152256 | tf_op jit(solution)/shard_map/dot_general | solution.py:96
  16.7 0.1 reduce_sum.62
  16.8 0.1 reduce_sum.63
  16.9 32.7 %psum.14 = f32[32]{0:T(128)S(1)} all-reduce(f32[32]{0:T(128)S(1)} %reduce_sum.63), channel_id=1, replica_groups=mesh['dp'=2,'seq'=16] {'seq'}, use_global_device_ids=true, to_apply=%region_2.3 | all-reduce | flops 32 | bytes 256 | tf_op jit(solution)/shard_map/psum | solution.py:102
  49.6 0.1 broadcast_in_dim.14
  49.7 0.1 sub.20
  49.8 0.2 multiply_reduce_fusion.2
  50.0 0.1 reduce_sum.65
  50.1 0.1 reduce_sum.66
  50.2 29.5 %psum.15 = f32[32]{0:T(128)S(1)} all-reduce(f32[32]{0:T(128)S(1)} %reduce_sum.66), channel_id=1, replica_groups=mesh['dp'=2,'seq'=16] {'seq'}, use_global_device_ids=true, to_apply=%region_5.6 | all-reduce | flops 32 | bytes 256 | tf_op jit(solution)/shard_map/psum | solution.py:105
  79.8 0.1 broadcast_in_dim.15
  79.8 0.1 mul.57
  80.0 0.5 fusion.81
  80.4 0.1 multiply_reduce_fusion.1
  80.5 0.1 multiply_convert_fusion
  80.7 0.3 convolution_convert_fusion.1
  81.0 0.1 reshape_reshape.10
  81.1 0.8 reshape.134
  81.9 3.5 %all-to-all-start.1 = ((bf16[16,2,1280]{2,1,0:T(2,128)(2,1)}), bf16[16,2,1280]{2,1,0:T(2,128)(2,1)S(1)}, u32[]{:S(2)}, u32[]{:S(2)}) async-start(bf16[16,2,1280]{2,1,0:T(2,128)(2,1)} %reshape.134), calls=%async_computation.1 | async-start | bytes 163840 | tf_op jit(solution)/shard_map/all_to_all | solution.py:138
  85.4 0.3 convolution_convert_fusion.2
  85.7 6.8 %all-to-all-done.1 = bf16[16,2,1280]{2,1,0:T(2,128)(2,1)S(1)} async-done(((bf16[16,2,1280]{2,1,0:T(2,128)(2,1)}), bf16[16,2,1280]{2,1,0:T(2,128)(2,1)S(1)}, u32[]{:S(2)}, u32[]{:S(2)}) %all-to-all-start.1) | async-done | bytes 81952 | tf_op jit(solution)/shard_map/all_to_all | solution.py:138
  92.5 0.7 broadcast_in_dim.19
  93.2 3.5 %all-to-all-start = ((bf16[16,128,40]{1,2,0:T(8,128)(2,1)}), bf16[16,128,40]{1,2,0:T(8,128)(2,1)S(1)}, u32[]{:S(2)}, u32[]{:S(2)}) async-start(bf16[16,128,40]{1,2,0:T(8,128)(2,1)} %bitcast.18), calls=%async_computation | async-start | bytes 327680 | tf_op jit(solution)/shard_map/all_to_all | solution.py:140
  96.7 0.3 convolution_convert_fusion
  97.0 8.1 %all-to-all-done = bf16[16,128,40]{1,2,0:T(8,128)(2,1)S(1)} async-done(((bf16[16,128,40]{1,2,0:T(8,128)(2,1)}), bf16[16,128,40]{1,2,0:T(8,128)(2,1)S(1)}, u32[]{:S(2)}, u32[]{:S(2)}) %all-to-all-start) | async-done | bytes 163872 | tf_op jit(solution)/shard_map/all_to_all | solution.py:140
  105.1 0.7 broadcast_in_dim.20
  105.8 3.5 %all-to-all-start.2 = ((bf16[16,128,40]{1,2,0:T(8,128)(2,1)}), bf16[16,128,40]{1,2,0:T(8,128)(2,1)S(1)}, u32[]{:S(2)}, u32[]{:S(2)}) async-start(bf16[16,128,40]{1,2,0:T(8,128)(2,1)} %bitcast.24), calls=%async_computation.2 | async-start | bytes 327680 | tf_op jit(solution)/shard_map/all_to_all | solution.py:141
  109.3 0.2 reshape.135
  109.5 0.2 reshape.125
  109.7 0.3 copy.79
  110.0 7.7 %all-to-all-done.2 = bf16[16,128,40]{1,2,0:T(8,128)(2,1)S(1)} async-done(((bf16[16,128,40]{1,2,0:T(8,128)(2,1)}), bf16[16,128,40]{1,2,0:T(8,128)(2,1)S(1)}, u32[]{:S(2)}, u32[]{:S(2)}) %all-to-all-start.2) | async-done | bytes 163872 | tf_op jit(solution)/shard_map/all_to_all | solution.py:141
  117.7 0.3 copy.80
  118.0 13.9 %while.15 = (s32[]{:T(128)}, f32[1,1024]{1,0:T(1,128)S(1)}, f32[1,1024]{1,0:T(1,128)S(1)}, f32[1024,1,40]{0,2,1:T(8,128)S(1)}, bf16[2,1024,40]{2,1,0:T(8,128)(2,...) while((s32[]{:T(128)}, f32[1,1024]{1,0:T(1,128)S(1)}, ...), condition=%wide.region_11.12_spmd.clone, body=%wide.region_8.0_spmd.clone.sunk | while | flops 176288768 | bytes 30359692 | solution.py:70
  118.0 2.6 %multiply_reduce_fusion.4 = (f32[1024]{0:T(1024)S(1)}, f32[1024,1024]{1,0:T(8,128)}) fusion(bf16[1024,1,40]{0,2,1:T(8,128)(2,1)S(1)} %get-tuple-element.172, bf16[2,1024,40]{2,1,0:T(8,128)(2,1)S(1)} %get-tuple-element.171, s32[]{:T(128)} %get-tuple-element.158), kind=kOutput, calls=%fused_computation.1.clone.1 | convolution fusion | flops 85982208 | bytes 4542468 | tf_op jit(solution)/shard_map/while/body/eval_jaxpr/qhd,khd->hqk/dot_general | solution.py:55
  120.7 3.1 %fusion.105 = f32[1024]{0:T(1024)S(1)} fusion(f32[1024,1024]{1,0:T(8,128)} %get-tuple-element.146, f32[1024]{0:T(1024)S(1)} %bitcast.150), kind=kLoop, calls=%fused_computation.3.clone.1 | loop fusion | flops 3144704 | bytes 4202496 | tf_op jit(solution)/shard_map/while/body/eval_jaxpr/reduce_sum | solution.py:61
  123.8 0.3 copy-done.1
  124.1 0.8 fusion.107
  125.0 2.6 %multiply_reduce_fusion.4 = (f32[1024]{0:T(1024)S(1)}, f32[1024,1024]{1,0:T(8,128)}) fusion(bf16[1024,1,40]{0,2,1:T(8,128)(2,1)S(1)} %get-tuple-element.172, bf16[2,1024,40]{2,1,0:T(8,128)(2,1)S(1)} %get-tuple-element.171, s32[]{:T(128)} %get-tuple-element.158), kind=kOutput, calls=%fused_computation.1.clone.1 | convolution fusion | flops 85982208 | bytes 4542468 | tf_op jit(solution)/shard_map/while/body/eval_jaxpr/qhd,khd->hqk/dot_general | solution.py:55
  127.6 3.1 %fusion.105 = f32[1024]{0:T(1024)S(1)} fusion(f32[1024,1024]{1,0:T(8,128)} %get-tuple-element.146, f32[1024]{0:T(1024)S(1)} %bitcast.150), kind=kLoop, calls=%fused_computation.3.clone.1 | loop fusion | flops 3144704 | bytes 4202496 | tf_op jit(solution)/shard_map/while/body/eval_jaxpr/reduce_sum | solution.py:61
  130.7 0.3 copy-done.1
  131.0 0.8 fusion.107
  132.0 0.2 reshape.128
  132.2 0.2 reshape.136
  132.3 9.7 %all_to_all.20 = bf16[16,2,1280]{2,1,0:T(2,128)(2,1)S(1)} all-to-all(bf16[16,2,1280]{2,1,0:T(2,128)(2,1)S(1)} %reshape.136), channel_id=1, replica_groups=mesh['dp'=2,'seq'=16] {'seq'}, dimensions={0} | all-to-all | bytes 163840 | tf_op jit(solution)/shard_map/all_to_all | solution.py:161
  142.0 0.2 reshape.137
  142.2 0.1 copy.78
  142.3 0.1 reshape.130
  142.5 1.1 fusion.28
  (45 shorter events, 0.3 us)
Async XLA Ops:
  0.0 15.0 %copy-start = (bf16[320,320]{1,0:T(8,128)(2,1)S(1)}, bf16[320,320]{1,0:T(8,128)(2,1)}, u32[]{:S(2)}) copy-start(bf16[320,320]{1,0:T(8,128)(2,1)} %param.20) | copy-start | bytes 614404
  0.0 12.5 %copy-start.2 = (bf16[3,3,320,320]{3,2,1,0:T(8,128)(2,1)S(1)}, bf16[3,3,320,320]{3,2,1,0:T(8,128)(2,1)}, u32[]{:S(2)}) copy-start(bf16[3,3,320,320]{3,2,1,0:T(8,128)(2,1)} %param.18) | copy-start | bytes 5529604
  0.0 4.0 %collective-permute-start = (bf16[128,320]{0,1:T(8,128)(2,1)}, bf16[128,320]{0,1:T(8,128)(2,1)S(1)}, u32[]{:S(2)}, u32[]{:S(2)}) collective-permute-start(bf16[128,320]{0,1:T(8,128)(2,1)} %param.17), channel_id=1, source_target_pairs={{0,1},{1,2},{2,3},{3,4},{4,5},{5,6},{6,7},{7,8},{8,9},{9,10},{10,1... | collective-permute-start | bytes 245768 | tf_op jit(solution)/shard_map/ppermute | solution.py:19
  2.7 5.5 %collective-permute-start.1 = (bf16[128,320]{0,1:T(8,128)(2,1)}, bf16[128,320]{0,1:T(8,128)(2,1)S(1)}, u32[]{:S(2)}, u32[]{:S(2)}) collective-permute-start(bf16[128,320]{0,1:T(8,128)(2,1)} %param.17), channel_id=1, source_target_pairs={{1,0},{2,1},{3,2},{4,3},{5,4},{6,5},{7,6},{8,7},{9,8},{10,9},{11,1... | collective-permute-start | bytes 245768 | tf_op jit(solution)/shard_map/ppermute | solution.py:22
  8.1 1.2 copy-start.10
  9.1 4.3 %copy-start.3 = (bf16[128,320]{0,1:T(8,128)(2,1)S(1)}, bf16[128,320]{0,1:T(8,128)(2,1)}, u32[]{:S(2)}) copy-start(bf16[128,320]{0,1:T(8,128)(2,1)} %param.17) | copy-start | bytes 245764
  12.8 2.2 %copy-start.13 = (f32[320]{0:T(512)S(1)}, f32[320]{0:T(512)}, u32[]{:S(2)}) copy-start(f32[320]{0:T(512)} %param.21) | copy-start | bytes 3844
  12.8 2.2 %copy-start.14 = (f32[320]{0:T(512)S(1)}, f32[320]{0:T(512)}, u32[]{:S(2)}) copy-start(f32[320]{0:T(512)} %param.19) | copy-start | bytes 3844
  13.4 66.6 %copy-start.4 = (bf16[320,320]{1,0:T(8,128)(2,1)S(1)}, bf16[320,320]{1,0:T(8,128)(2,1)}, u32[]{:S(2)}) copy-start(bf16[320,320]{1,0:T(8,128)(2,1)} %param.23) | copy-start | bytes 614404
  13.4 66.6 %copy-start.11 = (f32[320]{0:T(512)S(1)}, f32[320]{0:T(512)}, u32[]{:S(2)}) copy-start(f32[320]{0:T(512)} %param.22) | copy-start | bytes 3844
  13.7 66.8 %copy-start.12 = (f32[320]{0:T(512)S(1)}, f32[320]{0:T(512)}, u32[]{:S(2)}) copy-start(f32[320]{0:T(512)} %param.24) | copy-start | bytes 3844
  13.7 66.9 %copy-start.5 = (bf16[320,320]{1,0:T(8,128)(2,1)S(1)}, bf16[320,320]{1,0:T(8,128)(2,1)}, u32[]{:S(2)}) copy-start(bf16[320,320]{1,0:T(8,128)(2,1)} %param.25) | copy-start | bytes 614404
  15.0 70.5 %copy-start.6 = (bf16[320,320]{1,0:T(8,128)(2,1)S(1)}, bf16[320,320]{1,0:T(8,128)(2,1)}, u32[]{:S(2)}) copy-start(bf16[320,320]{1,0:T(8,128)(2,1)} %param.26) | copy-start | bytes 614404
  16.7 80.0 %copy-start.7 = (bf16[320,320]{1,0:T(8,128)(2,1)S(1)}, bf16[320,320]{1,0:T(8,128)(2,1)}, u32[]{:S(2)}) copy-start(bf16[320,320]{1,0:T(8,128)(2,1)} %param.27) | copy-start | bytes 614404
  81.9 10.6 %all-to-all-start.1 = ((bf16[16,2,1280]{2,1,0:T(2,128)(2,1)}), bf16[16,2,1280]{2,1,0:T(2,128)(2,1)S(1)}, u32[]{:S(2)}, u32[]{:S(2)}) async-start(bf16[16,2,1280]{2,1,0:T(2,128)(2,1)} %reshape.134), calls=%async_computation.1 | async-start | bytes 163840 | tf_op jit(solution)/shard_map/all_to_all | solution.py:138
  93.2 11.9 %all-to-all-start = ((bf16[16,128,40]{1,2,0:T(8,128)(2,1)}), bf16[16,128,40]{1,2,0:T(8,128)(2,1)S(1)}, u32[]{:S(2)}, u32[]{:S(2)}) async-start(bf16[16,128,40]{1,2,0:T(8,128)(2,1)} %bitcast.18), calls=%async_computation | async-start | bytes 327680 | tf_op jit(solution)/shard_map/all_to_all | solution.py:140
  105.8 11.9 %all-to-all-start.2 = ((bf16[16,128,40]{1,2,0:T(8,128)(2,1)}), bf16[16,128,40]{1,2,0:T(8,128)(2,1)S(1)}, u32[]{:S(2)}, u32[]{:S(2)}) async-start(bf16[16,128,40]{1,2,0:T(8,128)(2,1)} %bitcast.24), calls=%async_computation.2 | async-start | bytes 327680 | tf_op jit(solution)/shard_map/all_to_all | solution.py:141
  120.7 3.4 %copy-start.1 = (f32[1024,1024]{1,0:T(8,128)S(1)}, f32[1024,1024]{1,0:T(8,128)}, u32[]{:S(2)}) copy-start(f32[1024,1024]{1,0:T(8,128)} %get-tuple-element.146) | copy-start | bytes 12582916 | tf_op jit(solution)/shard_map/while
  127.6 3.4 %copy-start.1 = (f32[1024,1024]{1,0:T(8,128)S(1)}, f32[1024,1024]{1,0:T(8,128)}, u32[]{:S(2)}) copy-start(f32[1024,1024]{1,0:T(8,128)} %get-tuple-element.146) | copy-start | bytes 12582916 | tf_op jit(solution)/shard_map/while
  131.9 10.6 %copy-start.8 = (bf16[320,320]{1,0:T(8,128)(2,1)S(1)}, bf16[320,320]{1,0:T(8,128)(2,1)}, u32[]{:S(2)}) copy-start(bf16[320,320]{1,0:T(8,128)(2,1)} %param.29) | copy-start | bytes 614404
  131.9 10.6 %copy-start.9 = (bf16[320,320]{1,0:T(8,128)(2,1)S(1)}, bf16[320,320]{1,0:T(8,128)(2,1)}, u32[]{:S(2)}) copy-start(bf16[320,320]{1,0:T(8,128)(2,1)} %param.28) | copy-start | bytes 614404
where the time goes:
time: 144 us
  blocking collectives  71.9 us (50%)
  waiting for transfers between devices  26.7 us (19%)
  matrix products  16.6 us (12%)
  starting transfers between devices  14.5 us (10%)
  other arithmetic  7.84 us (5%)
  local copies, waits for them, and re-layouts  5.58 us (4%)
    psum x1, blocking collectives, local(): mean_group = lax.psum(local_sum, 'seq') / entry_count  32.7 us
    psum x1, blocking collectives, local(): var_group = lax.psum(local_spread, 'seq') / entry_count  29.5 us
    all_to_all x1, blocking collectives, local(): lax.all_to_all(head_result, 'seq', split_axis=0, concat_axis=0, tiled=True)  9.7 us
    all_to_all x1, waiting for transfers between devices, local(): lax.all_to_all(copies_for(local_keys), 'seq', split_axis=0, concat_axis=0...  8.08 us
    all_to_all x1, waiting for transfers between devices, local(): lax.all_to_all(copies_for(local_values), 'seq', split_axis=0, concat_axis...  7.68 us
    all_to_all x1, waiting for transfers between devices, local(): lax.all_to_all(query_send, 'seq', split_axis=0, concat_axis=0, tiled=True)  6.76 us
    reduce_sum x2, other arithmetic, advance(): running_sum = running_sum * decay_by + jnp.sum(weights, axis=2)  6.15 us
    dot_general x8, matrix products, conv_extended(): jnp.dot(window, conv_weight[row_shift, col_shift], preferred_element_type...  5.47 us
  transfers between devices with their start and end apart: 5, of which 4 were waited for; matrix products, arithmetic and copies ran while one was open for 1% of the time, Pallas kernels for 0%

commit v1 on v0

--- a/solution.py
+++ b/solution.py
@@ -9,6 +9,28 @@
 WIDTH = 128
 norm_eps = 1e-06
 layer_eps = 1e-05
+
+
+def split_up(x, dim, peers):
+    before, after = (x.shape[:dim], x.shape[dim + 1 :])
+    return jnp.moveaxis(x.reshape(*before, peers, -1, *after), dim, 0)
+
+
+def in_order(blocks, dim):
+    lengths = list(blocks.shape[1:])
+    lengths[dim] *= blocks.shape[0]
+    return jnp.moveaxis(blocks, 0, dim).reshape(lengths)
+
+
+def pairwise_exchange(x, axis, split_dim, concat_dim):
+    size, index = (lax.axis_size(axis), lax.axis_index(axis))
+    tiles = split_up(x, split_dim, size)
+    outs = [tiles[index]]
+    for step in range(1, size):
+        sent = tiles[index ^ step]
+        outs.append(lax.ppermute(sent, axis, [(i, i ^ step) for i in range(size)]))
+    tiles = jnp.stack(outs)[index ^ jnp.arange(size)]
+    return in_order(tiles, concat_dim)
 
 
 def with_halo(block, sides, width):
@@ -138,7 +160,7 @@
     own_queries = lax.all_to_all(query_send, "seq", split_axis=0, concat_axis=0, tiled=True)
     head_keys, head_values = (
         lax.all_to_all(copies_for(local_keys), "seq", split_axis=0, concat_axis=0, tiled=True),
-        lax.all_to_all(copies_for(local_values), "seq", split_axis=0, concat_axis=0, tiled=True),
+        pairwise_exchange(copies_for(local_values), "seq", 0, 0),
     )
     query_rows = own_queries.shape[0] * sub_rows
     own_queries = own_queries.reshape(query_rows, 1, head_dim)

time: 144 us -> 149 us (1.035)
  starting transfers between devices: 14.5 us -> 33.9 us
  waiting for transfers between devices: 26.7 us -> 11.2 us
    ppermute x0 -> x15, starting transfers between devices: none -> 20.7 us  [pairwise_exchange(): outs.append(lax.ppermute(sent, axis, [(i, i ^ step) for i in range(size)]))]
    all_to_all x1 -> x0, waiting for transfers between devices: 7.68 us -> none  [local(): lax.all_to_all(copies_for(local_values), 'seq', split_axis=0, concat_axis...]
    all_to_all x1, waiting for transfers between devices: 6.76 us -> 0.01 us  [local(): lax.all_to_all(query_send, 'seq', split_axis=0, concat_axis=0, tiled=True)]
    all_to_all x1 -> x0, starting transfers between devices: 3.52 us -> none  [local(): lax.all_to_all(copies_for(local_values), 'seq', split_axis=0, concat_axis...]
    all_to_all x1, starting transfers between devices: 3.52 us -> 5.74 us  [local(): lax.all_to_all(copies_for(local_keys), 'seq', split_axis=0, concat_axis=0...]
  transfers between devices with their start and end apart: 5 -> 19, of which waited for: 4 -> 2; matrix products, arithmetic and copies ran while one was open for 1% -> 2% of each run, Pallas kernels for 0% -> 0%
where the time goes in v1:
time: 149 us
  blocking collectives  71.9 us (48%)
  starting transfers between devices  33.9 us (23%)
  matrix products  16.9 us (11%)
  waiting for transfers between devices  11.2 us (8%)
  other arithmetic  7.84 us (5%)
  local copies, waits for them, and re-layouts  6.28 us (4%)
    psum x1, blocking collectives, local(): mean_group = lax.psum(local_sum, 'seq') / entry_count  32.7 us
    psum x1, blocking collectives, local(): var_group = lax.psum(local_spread, 'seq') / entry_count  29.5 us
    ppermute x15, starting transfers between devices, pairwise_exchange(): outs.append(lax.ppermute(sent, axis, [(i, i ^ step) for i in range(size)]))  20.7 us
    all_to_all x1, blocking collectives, local(): lax.all_to_all(head_result, 'seq', split_axis=0, concat_axis=0, tiled=True)  9.7 us
    all_to_all x1, waiting for transfers between devices, local(): lax.all_to_all(copies_for(local_keys), 'seq', split_axis=0, concat_axis=0...  7.14 us
    reduce_sum x2, other arithmetic, advance(): running_sum = running_sum * decay_by + jnp.sum(weights, axis=2)  6.15 us
    all_to_all x1, starting transfers between devices, local(): lax.all_to_all(copies_for(local_keys), 'seq', split_axis=0, concat_axis=0...  5.74 us
    dot_general x2, matrix products, advance(): jnp.einsum('qhd,khd->hqk', queries, keys_block, preferred_element_type=jn...  5.29 us
  transfers between devices with their start and end apart: 19, of which 2 were waited for; matrix products, arithmetic and copies ran while one was open for 2% of the time, Pallas kernels for 0%

profile of v1, /device:TPU:0, one launch (start us, length us, event | category | flops | bytes accessed | tf_op | source)
XLA Modules:
  0.0 148.7 jit_solution(14200220141715511863)
XLA Ops:
  0.0 2.7 %collective-permute-start = (bf16[128,320]{0,1:T(8,128)(2,1)}, bf16[128,320]{0,1:T(8,128)(2,1)S(1)}, u32[]{:S(2)}, u32[]{:S(2)}) collective-permute-start(bf16[128,320]{0,1:T(8,128)(2,1)} %param.17), channel_id=1, source_target_pairs={{0,1},{1,2},{2,3},{3,4},{4,5},{5,6},{6,7},{7,8},{8,9},{9,10},{10,1... | collective-permute-start | bytes 245768 | tf_op jit(solution)/shard_map/ppermute | solution.py:41
  2.7 1.3 collective-permute-start.1
  4.2 4.0 %collective-permute-done.1 = bf16[128,320]{0,1:T(8,128)(2,1)S(1)} collective-permute-done((bf16[128,320]{0,1:T(8,128)(2,1)}, bf16[128,320]{0,1:T(8,128)(2,1)S(1)}, u32[]{:S(2)}, u32[]{:S(2)}) %collective-permute-start.1) | collective-permute-done | bytes 81952 | tf_op jit(solution)/shard_map/ppermute | solution.py:44
  8.1 0.6 copy-done.9
  8.8 0.9 pad_maximum_fusion
  9.7 0.2 copy.64
  9.9 1.2 fusion.39
  11.2 1.9 %fusion.30 = f32[128,320]{0,1:T(8,128)} fusion(bf16[3,3,320,320]{3,2,1,0:T(8,128)(2,1)} %param.18, bf16[3,128,320]{2,1,0:T(8,128)(2,1)S(1)} %bitcast.206), kind=kOutput, calls=%fused_computation.47 | convolution fusion | flops 26214400 | bytes 655360 | tf_op jit(solution)/shard_map/dot_general | solution.py:59
  13.1 0.3 convolution_add_fusion.9
  13.4 0.3 convolution_add_fusion.8
  13.7 0.3 convolution_add_fusion.7
  14.0 0.3 convolution_add_fusion.6
  14.3 0.3 convolution_add_fusion.5
  14.6 0.3 convolution_add_fusion.4
  15.0 1.7 %fusion.79 = (f32[320]{0:T(512)S(1)}, f32[128,320]{0,1:T(8,128)S(1)}) fusion(f32[320]{0:T(512)S(1)} %copy-done.12, bf16[320,320]{1,0:T(8,128)(2,1)S(1)} %copy-done, f32[128,320]{0,1:T(8,128)} %fusion.30, f32[128,320]{0,1:T(8,128)S(1)} %convolution_add_fusion.4, bf16[128,320]{0,1:T(8,128)(2,1)} %copy-done.9, bf16[3,3,320,320]{3,2,1,0:T(8,128)(2,1)S(1)} %copy-done.2, ...), kind=kOutput, calls=%fused_computation.135 | convolution fusion | flops 53001920 | bytes 1152256 | tf_op jit(solution)/shard_map/dot_general | solution.py:118
  16.7 0.1 reduce_sum.63
  16.8 32.7 %psum.14 = f32[32]{0:T(128)S(1)} all-reduce(f32[32]{0:T(128)S(1)} %reduce_sum.63), channel_id=1, replica_groups=mesh['dp'=2,'seq'=16] {'seq'}, use_global_device_ids=true, to_apply=%region_2.3 | all-reduce | flops 32 | bytes 256 | tf_op jit(solution)/shard_map/psum | solution.py:124
  49.6 0.1 sub.20
  49.7 0.2 multiply_reduce_fusion.2
  49.9 0.1 reduce_sum.65
  50.0 0.1 reduce_sum.66
  50.2 29.5 %psum.15 = f32[32]{0:T(128)S(1)} all-reduce(f32[32]{0:T(128)S(1)} %reduce_sum.66), channel_id=1, replica_groups=mesh['dp'=2,'seq'=16] {'seq'}, use_global_device_ids=true, to_apply=%region_5.6 | all-reduce | flops 32 | bytes 256 | tf_op jit(solution)/shard_map/psum | solution.py:127
  79.7 0.1 mul.57
  79.9 0.5 fusion.82
  80.4 0.1 multiply_convert_fusion
  80.6 1.2 convolution_convert_fusion
  82.1 1.8 %collective-permute-start.4 = (bf16[1,128,40]{1,2,0:T(8,128)(2,1)S(1)}, bf16[1,128,40]{1,2,0:T(8,128)(2,1)S(1)}, u32[]{:S(2)}, u32[]{:S(2)}) collective-permute-start(bf16[1,128,40]{1,2,0:T(8,128)(2,1)S(1)} %get-tuple-element.106), channel_id=1, source_target_pairs={{0,3},{1,2},{2,1},{3,0},{4,7},{5,6},{6,5},{7,4},{8,11},{9,10},{10,... | collective-permute-start | bytes 30728 | tf_op jit(solution)/shard_map/ppermute | solution.py:31
  83.9 1.7 %collective-permute-start.6 = (bf16[1,128,40]{1,2,0:T(8,128)(2,1)S(1)}, bf16[1,128,40]{1,2,0:T(8,128)(2,1)S(1)}, u32[]{:S(2)}, u32[]{:S(2)}) collective-permute-start(bf16[1,128,40]{1,2,0:T(8,128)(2,1)S(1)} %get-tuple-element.104), channel_id=1, source_target_pairs={{0,5},{1,4},{2,7},{3,6},{4,1},{5,0},{6,3},{7,2},{8,13},{9,12},{10,... | collective-permute-start | bytes 30728 | tf_op jit(solution)/shard_map/ppermute | solution.py:31
  85.6 0.3 convolution_convert_fusion.1
  85.9 0.1 reshape_reshape.10
  86.0 0.8 reshape.157
  86.8 3.5 %all-to-all-start.1 = ((bf16[16,2,1280]{2,1,0:T(2,128)(2,1)}), bf16[16,2,1280]{2,1,0:T(2,128)(2,1)S(1)}, u32[]{:S(2)}, u32[]{:S(2)}) async-start(bf16[16,2,1280]{2,1,0:T(2,128)(2,1)} %reshape.157), calls=%async_computation.1 | async-start | bytes 163840 | tf_op jit(solution)/shard_map/all_to_all | solution.py:160
  90.4 0.3 convolution_convert_fusion.2
  90.7 2.8 %collective-permute-start.7 = (bf16[1,128,40]{1,2,0:T(8,128)(2,1)S(1)}, bf16[1,128,40]{1,2,0:T(8,128)(2,1)S(1)}, u32[]{:S(2)}, u32[]{:S(2)}) collective-permute-start(bf16[1,128,40]{1,2,0:T(8,128)(2,1)S(1)} %get-tuple-element.103), channel_id=1, source_target_pairs={{0,6},{1,7},{2,4},{3,5},{4,2},{5,3},{6,0},{7,1},{8,14},{9,15},{10,... | collective-permute-start | bytes 30728 | tf_op jit(solution)/shard_map/ppermute | solution.py:31
  93.5 2.5 %collective-permute-start.9 = (bf16[1,128,40]{1,2,0:T(8,128)(2,1)S(1)}, bf16[1,128,40]{1,2,0:T(8,128)(2,1)S(1)}, u32[]{:S(2)}, u32[]{:S(2)}) collective-permute-start(bf16[1,128,40]{1,2,0:T(8,128)(2,1)S(1)} %get-tuple-element.101), channel_id=1, source_target_pairs={{0,8},{1,9},{2,10},{3,11},{4,12},{5,13},{6,14},{7,15},{8,0},{9,1},... | collective-permute-start | bytes 30728 | tf_op jit(solution)/shard_map/ppermute | solution.py:31
  96.0 0.2 collective-permute-start.10
  96.3 3.5 %collective-permute-start.11 = (bf16[1,128,40]{1,2,0:T(8,128)(2,1)S(1)}, bf16[1,128,40]{1,2,0:T(8,128)(2,1)S(1)}, u32[]{:S(2)}, u32[]{:S(2)}) collective-permute-start(bf16[1,128,40]{1,2,0:T(8,128)(2,1)S(1)} %get-tuple-element.99), channel_id=1, source_target_pairs={{0,10},{1,11},{2,8},{3,9},{4,14},{5,15},{6,12},{7,13},{8,2},{9,3},... | collective-permute-start | bytes 30728 | tf_op jit(solution)/shard_map/ppermute | solution.py:31
  99.8 3.2 %collective-permute-start.13 = (bf16[1,128,40]{1,2,0:T(8,128)(2,1)S(1)}, bf16[1,128,40]{1,2,0:T(8,128)(2,1)S(1)}, u32[]{:S(2)}, u32[]{:S(2)}) collective-permute-start(bf16[1,128,40]{1,2,0:T(8,128)(2,1)S(1)} %get-tuple-element.97), channel_id=1, source_target_pairs={{0,12},{1,13},{2,14},{3,15},{4,8},{5,9},{6,10},{7,11},{8,4},{9,5},... | collective-permute-start | bytes 30728 | tf_op jit(solution)/shard_map/ppermute | solution.py:31
  103.1 0.4 collective-permute-start.14
  103.4 4.4 %collective-permute-start.15 = (bf16[1,128,40]{1,2,0:T(8,128)(2,1)S(1)}, bf16[1,128,40]{1,2,0:T(8,128)(2,1)S(1)}, u32[]{:S(2)}, u32[]{:S(2)}) collective-permute-start(bf16[1,128,40]{1,2,0:T(8,128)(2,1)S(1)} %get-tuple-element.95), channel_id=1, source_target_pairs={{0,14},{1,15},{2,12},{3,13},{4,10},{5,11},{6,8},{7,9},{8,6},{9,7},... | collective-permute-start | bytes 30728 | tf_op jit(solution)/shard_map/ppermute | solution.py:31
  108.0 0.7 broadcast_in_dim.19
  108.7 5.7 %all-to-all-start = ((bf16[16,128,40]{1,2,0:T(8,128)(2,1)}), bf16[16,128,40]{1,2,0:T(8,128)(2,1)S(1)}, u32[]{:S(2)}, u32[]{:S(2)}) async-start(bf16[16,128,40]{1,2,0:T(8,128)(2,1)} %bitcast.18), calls=%async_computation | async-start | bytes 327680 | tf_op jit(solution)/shard_map/all_to_all | solution.py:162
  114.5 0.6 gather_fusion
  115.0 0.3 copy.80
  115.3 0.2 reshape.158
  115.5 0.2 reshape.138
  115.7 7.1 %all-to-all-done = bf16[16,128,40]{1,2,0:T(8,128)(2,1)S(1)} async-done(((bf16[16,128,40]{1,2,0:T(8,128)(2,1)}), bf16[16,128,40]{1,2,0:T(8,128)(2,1)S(1)}, u32[]{:S(2)}, u32[]{:S(2)}) %all-to-all-start) | async-done | bytes 163872 | tf_op jit(solution)/shard_map/all_to_all | solution.py:162
  122.8 0.3 copy.79
  123.1 13.9 %while.15 = (s32[]{:T(128)}, f32[1,1024]{1,0:T(1,128)S(1)}, f32[1,1024]{1,0:T(1,128)S(1)}, f32[1024,1,40]{0,2,1:T(8,128)S(1)}, bf16[2,1024,40]{2,1,0:T(8,128)(2,...) while((s32[]{:T(128)}, f32[1,1024]{1,0:T(1,128)S(1)}, ...), condition=%wide.region_11.12_spmd.clone, body=%wide.region_8.0_spmd.clone.sunk | while | flops 176288768 | bytes 30359692 | solution.py:92
  123.1 2.6 %multiply_reduce_fusion.4 = (f32[1024]{0:T(1024)S(1)}, f32[1024,1024]{1,0:T(8,128)}) fusion(bf16[1024,1,40]{0,2,1:T(8,128)(2,1)S(1)} %get-tuple-element.188, bf16[2,1024,40]{2,1,0:T(8,128)(2,1)S(1)} %get-tuple-element.187, s32[]{:T(128)} %get-tuple-element.174), kind=kOutput, calls=%fused_computation.2.clone.1 | convolution fusion | flops 85982208 | bytes 4542468 | tf_op jit(solution)/shard_map/while/body/eval_jaxpr/qhd,khd->hqk/dot_general | solution.py:77
  125.8 3.1 %fusion.106 = f32[1024]{0:T(1024)S(1)} fusion(f32[1024,1024]{1,0:T(8,128)} %get-tuple-element.162, f32[1024]{0:T(1024)S(1)} %bitcast.213), kind=kLoop, calls=%fused_computation.4.clone.1 | loop fusion | flops 3144704 | bytes 4202496 | tf_op jit(solution)/shard_map/while/body/eval_jaxpr/reduce_sum | solution.py:83
  128.9 0.3 copy-done.1
  129.2 0.8 fusion.108
  130.1 2.6 %multiply_reduce_fusion.4 = (f32[1024]{0:T(1024)S(1)}, f32[1024,1024]{1,0:T(8,128)}) fusion(bf16[1024,1,40]{0,2,1:T(8,128)(2,1)S(1)} %get-tuple-element.188, bf16[2,1024,40]{2,1,0:T(8,128)(2,1)S(1)} %get-tuple-element.187, s32[]{:T(128)} %get-tuple-element.174), kind=kOutput, calls=%fused_computation.2.clone.1 | convolution fusion | flops 85982208 | bytes 4542468 | tf_op jit(solution)/shard_map/while/body/eval_jaxpr/qhd,khd->hqk/dot_general | solution.py:77
  132.8 3.1 %fusion.106 = f32[1024]{0:T(1024)S(1)} fusion(f32[1024,1024]{1,0:T(8,128)} %get-tuple-element.162, f32[1024]{0:T(1024)S(1)} %bitcast.213), kind=kLoop, calls=%fused_computation.4.clone.1 | loop fusion | flops 3144704 | bytes 4202496 | tf_op jit(solution)/shard_map/while/body/eval_jaxpr/reduce_sum | solution.py:83
  135.9 0.3 copy-done.1
  136.2 0.8 fusion.108
  137.1 0.2 reshape.140
  137.3 0.2 reshape.159
  137.5 9.7 %all_to_all.15 = bf16[16,2,1280]{2,1,0:T(2,128)(2,1)S(1)} all-to-all(bf16[16,2,1280]{2,1,0:T(2,128)(2,1)S(1)} %reshape.159), channel_id=1, replica_groups=mesh['dp'=2,'seq'=16] {'seq'}, dimensions={0} | all-to-all | bytes 163840 | tf_op jit(solution)/shard_map/all_to_all | solution.py:183
  147.2 0.2 reshape.160
  147.3 0.1 copy.78
  147.5 0.1 reshape.142
  147.6 1.1 fusion.28
  (90 shorter events, 1.2 us)
Async XLA Ops:
  0.0 14.9 %copy-start = (bf16[320,320]{1,0:T(8,128)(2,1)S(1)}, bf16[320,320]{1,0:T(8,128)(2,1)}, u32[]{:S(2)}) copy-start(bf16[320,320]{1,0:T(8,128)(2,1)} %param.20) | copy-start | bytes 614404
  0.0 13.1 %copy-start.2 = (bf16[3,3,320,320]{3,2,1,0:T(8,128)(2,1)S(1)}, bf16[3,3,320,320]{3,2,1,0:T(8,128)(2,1)}, u32[]{:S(2)}) copy-start(bf16[3,3,320,320]{3,2,1,0:T(8,128)(2,1)} %param.18) | copy-start | bytes 5529604
  0.0 4.2 %collective-permute-start = (bf16[128,320]{0,1:T(8,128)(2,1)}, bf16[128,320]{0,1:T(8,128)(2,1)S(1)}, u32[]{:S(2)}, u32[]{:S(2)}) collective-permute-start(bf16[128,320]{0,1:T(8,128)(2,1)} %param.17), channel_id=1, source_target_pairs={{0,1},{1,2},{2,3},{3,4},{4,5},{5,6},{6,7},{7,8},{8,9},{9,10},{10,1... | collective-permute-start | bytes 245768 | tf_op jit(solution)/shard_map/ppermute | solution.py:41
  2.7 5.5 %collective-permute-start.1 = (bf16[128,320]{0,1:T(8,128)(2,1)}, bf16[128,320]{0,1:T(8,128)(2,1)S(1)}, u32[]{:S(2)}, u32[]{:S(2)}) collective-permute-start(bf16[128,320]{0,1:T(8,128)(2,1)} %param.17), channel_id=1, source_target_pairs={{1,0},{2,1},{3,2},{4,3},{5,4},{6,5},{7,6},{8,7},{9,8},{10,9},{11,1... | collective-permute-start | bytes 245768 | tf_op jit(solution)/shard_map/ppermute | solution.py:44
  8.1 0.6 copy-start.9
  9.7 4.3 %copy-start.3 = (bf16[128,320]{0,1:T(8,128)(2,1)S(1)}, bf16[128,320]{0,1:T(8,128)(2,1)}, u32[]{:S(2)}) copy-start(bf16[128,320]{0,1:T(8,128)(2,1)} %param.17) | copy-start | bytes 245764
  13.4 1.5 %copy-start.12 = (f32[320]{0:T(512)S(1)}, f32[320]{0:T(512)}, u32[]{:S(2)}) copy-start(f32[320]{0:T(512)} %param.21) | copy-start | bytes 3844
  13.4 1.5 %copy-start.13 = (f32[320]{0:T(512)S(1)}, f32[320]{0:T(512)}, u32[]{:S(2)}) copy-start(f32[320]{0:T(512)} %param.19) | copy-start | bytes 3844
  14.0 65.9 %copy-start.4 = (bf16[320,320]{1,0:T(8,128)(2,1)S(1)}, bf16[320,320]{1,0:T(8,128)(2,1)}, u32[]{:S(2)}) copy-start(bf16[320,320]{1,0:T(8,128)(2,1)} %param.23) | copy-start | bytes 614404
  14.0 65.9 %copy-start.10 = (f32[320]{0:T(512)S(1)}, f32[320]{0:T(512)}, u32[]{:S(2)}) copy-start(f32[320]{0:T(512)} %param.22) | copy-start | bytes 3844
  14.3 66.1 %copy-start.11 = (f32[320]{0:T(512)S(1)}, f32[320]{0:T(512)}, u32[]{:S(2)}) copy-start(f32[320]{0:T(512)} %param.24) | copy-start | bytes 3844
  14.9 70.6 %copy-start.5 = (bf16[320,320]{1,0:T(8,128)(2,1)S(1)}, bf16[320,320]{1,0:T(8,128)(2,1)}, u32[]{:S(2)}) copy-start(bf16[320,320]{1,0:T(8,128)(2,1)} %param.25) | copy-start | bytes 614404
  16.6 73.7 %copy-start.6 = (bf16[320,320]{1,0:T(8,128)(2,1)S(1)}, bf16[320,320]{1,0:T(8,128)(2,1)}, u32[]{:S(2)}) copy-start(bf16[320,320]{1,0:T(8,128)(2,1)} %param.26) | copy-start | bytes 614404
  81.9 8.7 %collective-permute-start.2 = (bf16[1,128,40]{1,2,0:T(8,128)(2,1)S(1)}, bf16[1,128,40]{1,2,0:T(8,128)(2,1)S(1)}, u32[]{:S(2)}, u32[]{:S(2)}) collective-permute-start(bf16[1,128,40]{1,2,0:T(8,128)(2,1)S(1)} %get-tuple-element.108), channel_id=1, source_target_pairs={{0,1},{1,0},{2,3},{3,2},{4,5},{5,4},{6,7},{7,6},{8,9},{9,8},{10,11... | collective-permute-start | bytes 30728 | tf_op jit(solution)/shard_map/ppermute | solution.py:31
  82.0 11.5 %collective-permute-start.3 = (bf16[1,128,40]{1,2,0:T(8,128)(2,1)S(1)}, bf16[1,128,40]{1,2,0:T(8,128)(2,1)S(1)}, u32[]{:S(2)}, u32[]{:S(2)}) collective-permute-start(bf16[1,128,40]{1,2,0:T(8,128)(2,1)S(1)} %get-tuple-element.107), channel_id=1, source_target_pairs={{0,2},{1,3},{2,0},{3,1},{4,6},{5,7},{6,4},{7,5},{8,10},{9,11},{10,... | collective-permute-start | bytes 30728 | tf_op jit(solution)/shard_map/ppermute | solution.py:31
  82.1 11.4 %collective-permute-start.4 = (bf16[1,128,40]{1,2,0:T(8,128)(2,1)S(1)}, bf16[1,128,40]{1,2,0:T(8,128)(2,1)S(1)}, u32[]{:S(2)}, u32[]{:S(2)}) collective-permute-start(bf16[1,128,40]{1,2,0:T(8,128)(2,1)S(1)} %get-tuple-element.106), channel_id=1, source_target_pairs={{0,3},{1,2},{2,1},{3,0},{4,7},{5,6},{6,5},{7,4},{8,11},{9,10},{10,... | collective-permute-start | bytes 30728 | tf_op jit(solution)/shard_map/ppermute | solution.py:31
  83.9 12.1 %collective-permute-start.5 = (bf16[1,128,40]{1,2,0:T(8,128)(2,1)S(1)}, bf16[1,128,40]{1,2,0:T(8,128)(2,1)S(1)}, u32[]{:S(2)}, u32[]{:S(2)}) collective-permute-start(bf16[1,128,40]{1,2,0:T(8,128)(2,1)S(1)} %get-tuple-element.105), channel_id=1, source_target_pairs={{0,4},{1,5},{2,6},{3,7},{4,0},{5,1},{6,2},{7,3},{8,12},{9,13},{10,... | collective-permute-start | bytes 30728 | tf_op jit(solution)/shard_map/ppermute | solution.py:31
  83.9 12.4 %collective-permute-start.6 = (bf16[1,128,40]{1,2,0:T(8,128)(2,1)S(1)}, bf16[1,128,40]{1,2,0:T(8,128)(2,1)S(1)}, u32[]{:S(2)}, u32[]{:S(2)}) collective-permute-start(bf16[1,128,40]{1,2,0:T(8,128)(2,1)S(1)} %get-tuple-element.104), channel_id=1, source_target_pairs={{0,5},{1,4},{2,7},{3,6},{4,1},{5,0},{6,3},{7,2},{8,13},{9,12},{10,... | collective-permute-start | bytes 30728 | tf_op jit(solution)/shard_map/ppermute | solution.py:31
  86.8 21.1 %all-to-all-start.1 = ((bf16[16,2,1280]{2,1,0:T(2,128)(2,1)}), bf16[16,2,1280]{2,1,0:T(2,128)(2,1)S(1)}, u32[]{:S(2)}, u32[]{:S(2)}) async-start(bf16[16,2,1280]{2,1,0:T(2,128)(2,1)} %reshape.157), calls=%async_computation.1 | async-start | bytes 163840 | tf_op jit(solution)/shard_map/all_to_all | solution.py:160
  90.7 9.1 %collective-permute-start.7 = (bf16[1,128,40]{1,2,0:T(8,128)(2,1)S(1)}, bf16[1,128,40]{1,2,0:T(8,128)(2,1)S(1)}, u32[]{:S(2)}, u32[]{:S(2)}) collective-permute-start(bf16[1,128,40]{1,2,0:T(8,128)(2,1)S(1)} %get-tuple-element.103), channel_id=1, source_target_pairs={{0,6},{1,7},{2,4},{3,5},{4,2},{5,3},{6,0},{7,1},{8,14},{9,15},{10,... | collective-permute-start | bytes 30728 | tf_op jit(solution)/shard_map/ppermute | solution.py:31
  93.5 6.3 %collective-permute-start.8 = (bf16[1,128,40]{1,2,0:T(8,128)(2,1)S(1)}, bf16[1,128,40]{1,2,0:T(8,128)(2,1)S(1)}, u32[]{:S(2)}, u32[]{:S(2)}) collective-permute-start(bf16[1,128,40]{1,2,0:T(8,128)(2,1)S(1)} %get-tuple-element.102), channel_id=1, source_target_pairs={{0,7},{1,6},{2,5},{3,4},{4,3},{5,2},{6,1},{7,0},{8,15},{9,14},{10,... | collective-permute-start | bytes 30728 | tf_op jit(solution)/shard_map/ppermute | solution.py:31
  93.5 9.5 %collective-permute-start.9 = (bf16[1,128,40]{1,2,0:T(8,128)(2,1)S(1)}, bf16[1,128,40]{1,2,0:T(8,128)(2,1)S(1)}, u32[]{:S(2)}, u32[]{:S(2)}) collective-permute-start(bf16[1,128,40]{1,2,0:T(8,128)(2,1)S(1)} %get-tuple-element.101), channel_id=1, source_target_pairs={{0,8},{1,9},{2,10},{3,11},{4,12},{5,13},{6,14},{7,15},{8,0},{9,1},... | collective-permute-start | bytes 30728 | tf_op jit(solution)/shard_map/ppermute | solution.py:31
  96.0 7.4 %collective-permute-start.10 = (bf16[1,128,40]{1,2,0:T(8,128)(2,1)S(1)}, bf16[1,128,40]{1,2,0:T(8,128)(2,1)S(1)}, u32[]{:S(2)}, u32[]{:S(2)}) collective-permute-start(bf16[1,128,40]{1,2,0:T(8,128)(2,1)S(1)} %get-tuple-element.100), channel_id=1, source_target_pairs={{0,9},{1,8},{2,11},{3,10},{4,13},{5,12},{6,15},{7,14},{8,1},{9,0},... | collective-permute-start | bytes 30728 | tf_op jit(solution)/shard_map/ppermute | solution.py:31
  96.3 11.6 %collective-permute-start.11 = (bf16[1,128,40]{1,2,0:T(8,128)(2,1)S(1)}, bf16[1,128,40]{1,2,0:T(8,128)(2,1)S(1)}, u32[]{:S(2)}, u32[]{:S(2)}) collective-permute-start(bf16[1,128,40]{1,2,0:T(8,128)(2,1)S(1)} %get-tuple-element.99), channel_id=1, source_target_pairs={{0,10},{1,11},{2,8},{3,9},{4,14},{5,15},{6,12},{7,13},{8,2},{9,3},... | collective-permute-start | bytes 30728 | tf_op jit(solution)/shard_map/ppermute | solution.py:31
  99.8 8.2 %collective-permute-start.12 = (bf16[1,128,40]{1,2,0:T(8,128)(2,1)S(1)}, bf16[1,128,40]{1,2,0:T(8,128)(2,1)S(1)}, u32[]{:S(2)}, u32[]{:S(2)}) collective-permute-start(bf16[1,128,40]{1,2,0:T(8,128)(2,1)S(1)} %get-tuple-element.98), channel_id=1, source_target_pairs={{0,11},{1,10},{2,9},{3,8},{4,15},{5,14},{6,13},{7,12},{8,3},{9,2},... | collective-permute-start | bytes 30728 | tf_op jit(solution)/shard_map/ppermute | solution.py:31
  99.8 8.1 %collective-permute-start.13 = (bf16[1,128,40]{1,2,0:T(8,128)(2,1)S(1)}, bf16[1,128,40]{1,2,0:T(8,128)(2,1)S(1)}, u32[]{:S(2)}, u32[]{:S(2)}) collective-permute-start(bf16[1,128,40]{1,2,0:T(8,128)(2,1)S(1)} %get-tuple-element.97), channel_id=1, source_target_pairs={{0,12},{1,13},{2,14},{3,15},{4,8},{5,9},{6,10},{7,11},{8,4},{9,5},... | collective-permute-start | bytes 30728 | tf_op jit(solution)/shard_map/ppermute | solution.py:31
  103.1 4.9 %collective-permute-start.14 = (bf16[1,128,40]{1,2,0:T(8,128)(2,1)S(1)}, bf16[1,128,40]{1,2,0:T(8,128)(2,1)S(1)}, u32[]{:S(2)}, u32[]{:S(2)}) collective-permute-start(bf16[1,128,40]{1,2,0:T(8,128)(2,1)S(1)} %get-tuple-element.96), channel_id=1, source_target_pairs={{0,13},{1,12},{2,15},{3,14},{4,9},{5,8},{6,11},{7,10},{8,5},{9,4},... | collective-permute-start | bytes 30728 | tf_op jit(solution)/shard_map/ppermute | solution.py:31
  103.4 11.0 %collective-permute-start.15 = (bf16[1,128,40]{1,2,0:T(8,128)(2,1)S(1)}, bf16[1,128,40]{1,2,0:T(8,128)(2,1)S(1)}, u32[]{:S(2)}, u32[]{:S(2)}) collective-permute-start(bf16[1,128,40]{1,2,0:T(8,128)(2,1)S(1)} %get-tuple-element.95), channel_id=1, source_target_pairs={{0,14},{1,15},{2,12},{3,13},{4,10},{5,11},{6,8},{7,9},{8,6},{9,7},... | collective-permute-start | bytes 30728 | tf_op jit(solution)/shard_map/ppermute | solution.py:31
  107.8 6.6 %collective-permute-start.16 = (bf16[1,128,40]{1,2,0:T(8,128)(2,1)S(1)}, bf16[1,128,40]{1,2,0:T(8,128)(2,1)S(1)}, u32[]{:S(2)}, u32[]{:S(2)}) collective-permute-start(bf16[1,128,40]{1,2,0:T(8,128)(2,1)S(1)} %get-tuple-element.94), channel_id=1, source_target_pairs={{0,15},{1,14},{2,13},{3,12},{4,11},{5,10},{6,9},{7,8},{8,7},{9,6},... | collective-permute-start | bytes 30728 | tf_op jit(solution)/shard_map/ppermute | solution.py:31
  108.7 14.2 %all-to-all-start = ((bf16[16,128,40]{1,2,0:T(8,128)(2,1)}), bf16[16,128,40]{1,2,0:T(8,128)(2,1)S(1)}, u32[]{:S(2)}, u32[]{:S(2)}) async-start(bf16[16,128,40]{1,2,0:T(8,128)(2,1)} %bitcast.18), calls=%async_computation | async-start | bytes 327680 | tf_op jit(solution)/shard_map/all_to_all | solution.py:162
  125.8 3.4 %copy-start.1 = (f32[1024,1024]{1,0:T(8,128)S(1)}, f32[1024,1024]{1,0:T(8,128)}, u32[]{:S(2)}) copy-start(f32[1024,1024]{1,0:T(8,128)} %get-tuple-element.162) | copy-start | bytes 12582916 | tf_op jit(solution)/shard_map/while
  132.7 3.4 %copy-start.1 = (f32[1024,1024]{1,0:T(8,128)S(1)}, f32[1024,1024]{1,0:T(8,128)}, u32[]{:S(2)}) copy-start(f32[1024,1024]{1,0:T(8,128)} %get-tuple-element.162) | copy-start | bytes 12582916 | tf_op jit(solution)/shard_map/while
  137.1 10.6 %copy-start.7 = (bf16[320,320]{1,0:T(8,128)(2,1)S(1)}, bf16[320,320]{1,0:T(8,128)(2,1)}, u32[]{:S(2)}) copy-start(bf16[320,320]{1,0:T(8,128)(2,1)} %param.29) | copy-start | bytes 614404
  137.1 10.5 %copy-start.8 = (bf16[320,320]{1,0:T(8,128)(2,1)S(1)}, bf16[320,320]{1,0:T(8,128)(2,1)}, u32[]{:S(2)}) copy-start(bf16[320,320]{1,0:T(8,128)(2,1)} %param.28) | copy-start | bytes 614404
